TPU v7x, 32 devices: a whole 2x2x4 slice. The times are simulated.
32 devices in a mesh: groups: 2 (over y), expert: 4 (over z), mp: 4 (over x, core).
Axes of the slice: x: 2, y: 2, z: 4, core: 2. Of those that a mesh axis runs over, the one named last changes fastest.
Arguments:
- tokens: bfloat16 [6144, 1024], P(('groups', 'expert'), 'mp'), parts along dimension 0, may hold values from -60 to 60
- gain: float32 [1024], replicated, may hold values from 0.1 to 1.9
- w_res_in: bfloat16 [1024, 4096], P(None, 'mp'), may hold values from -0.1875 to 0.1875
- w_res_out: bfloat16 [4096, 1024], P('mp'), may hold values from -0.09375 to 0.09375
- w_exp_in: bfloat16 [4, 1024, 4096], P('expert', None, 'mp'), may hold values from -0.1875 to 0.1875
- w_exp_out: bfloat16 [4, 4096, 1024], P('expert', 'mp'), may hold values from -0.09375 to 0.09375
- expert_of: int32 [6144], P(('groups', 'expert')), parts along dimension 0, may hold values from 0 to 3
- slot_of: int32 [6144], P(('groups', 'expert')), parts along dimension 0, may hold values from -1 to 239, as said below
- gate_prob: float32 [6144], P(('groups', 'expert')), parts along dimension 0, may hold values from 0.2 to 1
Outputs:
- layer_out: bfloat16 [6144, 1024], P(('groups', 'expert'), 'mp'), parts along dimension 0
There are 2 independent parts, one for each index of `groups`. A program takes and returns all parts, laid end to end along the dimension named above; an argument that names none is the same for every part. Nothing has to cross between parts.
Inputs may be any that keep to these rules, and one draw needn't show every extreme that they name: slot_of[t] is the number of earlier tokens of t's aligned block of 768 tokens with the same expert_of, or -1 where that number is 240 or more. In every draw one expert has more than 240 tokens in every aligned block.
All inputs are finite; a program needn't handle non-finite values.
Results may differ from a plain program's by a relative error of at most 0.014.
Values may be sent and summed in bfloat16 or wider, within the bound.
A program may use at most 64 MiB of HBM per device.

v0:
```python
import jax
import jax.numpy as jnp
from jax import lax
from jax.sharding import PartitionSpec as P


def rms_rows(tokens, gain):
    values = tokens.astype(jnp.float32)
    inverse = lax.rsqrt(jnp.mean(values * values, axis=-1, keepdims=True) + 1e-05)
    return (values * inverse * gain).astype(jnp.bfloat16)


def per_device(
    tokens, gain, w_res_in, w_res_out, w_exp_in, w_exp_out, expert_of, slot_of, gate_prob
):
    full_rows = lax.all_gather(tokens, "mp", axis=1, tiled=True)
    normed = rms_rows(full_rows, gain)
    res_hidden = jax.nn.gelu(jnp.dot(normed, w_res_in, preferred_element_type=jnp.float32)).astype(
        jnp.bfloat16
    )
    res_part = jnp.dot(res_hidden, w_res_out, preferred_element_type=jnp.float32)
    row_count = expert_of.shape[0]
    experts = lax.axis_size("expert")
    capacity = max(2, 5 * row_count // (4 * experts))
    feat_width = tokens.shape[1]
    slot_id = jnp.where(slot_of >= 0, expert_of * capacity + slot_of, -1)
    slot_index = jnp.arange(experts * capacity, dtype=jnp.int32)
    send_table = (slot_index[:, None] == slot_id[None, :]).astype(jnp.bfloat16)
    take_table = (slot_id[:, None] == slot_index[None, :]).astype(jnp.bfloat16)
    local_in = w_exp_in[0]
    local_out = w_exp_out[0]
    mp_index = lax.axis_index("mp")
    own_slice = lax.dynamic_slice_in_dim(normed, mp_index * feat_width, feat_width, 1)
    outgoing = jnp.dot(send_table, own_slice, preferred_element_type=jnp.float32).astype(
        jnp.bfloat16
    )
    incoming = lax.all_to_all(
        outgoing.reshape(experts, capacity, feat_width),
        "expert",
        split_axis=0,
        concat_axis=0,
        tiled=True,
    )
    piece = lax.all_gather(incoming, "mp", axis=2, tiled=True)
    flat_piece = piece.reshape(-1, piece.shape[2])
    preact = jnp.dot(flat_piece, local_in, preferred_element_type=jnp.float32)
    exp_hidden = jax.nn.gelu(preact).astype(jnp.bfloat16)
    exp_part = jnp.dot(exp_hidden, local_out, preferred_element_type=jnp.float32)
    gate_column = gate_prob[:, None]
    summed = lax.psum_scatter(exp_part.astype(jnp.bfloat16), "mp", scatter_dimension=1, tiled=True)
    returned = lax.all_to_all(
        summed.reshape(experts, capacity, feat_width),
        "expert",
        split_axis=0,
        concat_axis=0,
        tiled=True,
    )
    moe_value = jnp.dot(
        take_table,
        returned.reshape(experts * capacity, feat_width),
        preferred_element_type=jnp.float32,
    )
    res_sum = lax.psum_scatter(
        res_part.astype(jnp.bfloat16), "mp", scatter_dimension=1, tiled=True
    ).astype(jnp.float32)
    return (res_sum + gate_column * moe_value).astype(jnp.bfloat16)


def solution(mesh):
    return jax.shard_map(
        per_device,
        mesh=mesh,
        in_specs=(
            P(("groups", "expert"), "mp"),
            P(),
            P(None, "mp"),
            P("mp", None),
            P("expert", None, "mp"),
            P("expert", "mp", None),
            P(("groups", "expert")),
            P(("groups", "expert")),
            P(("groups", "expert")),
        ),
        out_specs=P(("groups", "expert"), "mp"),
        check_vma=False,
    )
```

profile of v0, /device:TPU:0, one launch (start us, length us, event | category | flops | bytes accessed | tf_op | source)
XLA Modules:
  0.0 153.2 jit_solution(7485082166365213157)
XLA Ops:
  6.5 0.0 copy-start
  6.5 0.0 all-gather.3.cloned.1.call-start
  6.5 0.7 all-gather.3.cloned.1.call-update
  7.3 0.0 all-gather.5.cloned.1.call-start
  7.3 0.7 add_select_fusion
  8.0 23.4 %all-gather.3.cloned.1.call-done = bf16[768,1024]{1,0:T(8,128)(2,1)} async-done(((bf16[768,256]{1,0:T(8,128)(2,1)}), bf16[768,1024]{1,0:T(8,128)(2,1)}) %all-gather.3.cloned.1.call-update) | async-done | bytes 1572880 | tf_op jit(solution)/shard_map/all_gather | solution.py:16
  31.5 1.9 %fusion.8 = f32[768]{0:T(1024)S(1)} fusion(bf16[768,1024]{1,0:T(8,128)(2,1)} %all-gather.3.cloned.1.call-done), kind=kLoop, calls=%fused_computation.12 | loop fusion | flops 2358528 | bytes 1575936 | tf_op jit(solution)/shard_map/reduce_sum | solution.py:9
  33.4 1.1 fusion.10
  34.5 1.1 copy-done.2
  35.6 0.6 fusion.39
  36.3 18.7 %all_to_all.10 = bf16[4,240,256]{2,1,0:T(8,128)(2,1)} all-to-all(bf16[4,240,256]{2,1,0:T(8,128)(2,1)S(1)} %bitcast.23), channel_id=1, replica_groups=mesh['groups'=2,'expert'=4,'mp'=4] {'expert'}, dimensions={0} | all-to-all | bytes 983040 | tf_op jit(solution)/shard_map/all_to_all | solution.py:37
  55.0 0.0 all-gather.5.cloned.1.call-update
  55.0 0.0 reduce-scatter.5.cloned.1.call-start
  55.1 20.3 %all-gather.5.cloned.1.call-done = bf16[4,240,1024]{2,1,0:T(8,128)(2,1)} async-done(((bf16[4,240,256]{2,1,0:T(8,128)(2,1)}), bf16[4,240,1024]{2,1,0:T(8,128)(2,1)}) %all-gather.5.cloned.1.call-update) | async-done | bytes 1966096 | tf_op jit(solution)/shard_map/all_gather | solution.py:44
  75.4 7.8 %fusion.27 = bf16[960,1024]{1,0:T(8,128)(2,1)} fusion(bf16[1,1024,1024]{2,1,0:T(8,128)(2,1)S(1)} %copy-done, bf16[960,1024]{1,0:T(8,128)(2,1)} %bitcast.24, bf16[1,1024,1024]{2,1,0:T(8,128)(2,1)} %param.13), kind=kOutput, calls=%fused_computation.31 | convolution fusion | flops 4036362240 | bytes 8126464 | tf_op jit(solution)/shard_map/dot_general | solution.py:48
  83.2 0.0 reduce-scatter.5.cloned.1.call-update
  83.2 0.0 reduce-scatter.3.cloned.1.call-start
  83.2 7.4 %convolution_convert_fusion = bf16[768,1024]{1,0:T(8,128)(2,1)} fusion(bf16[1024,1024]{1,0:T(8,128)(2,1)} %param.12, bf16[768,1024]{1,0:T(8,128)(2,1)} %copy-done.2, bf16[1024,1024]{1,0:T(8,128)(2,1)} %param.11), kind=kOutput, calls=%fused_computation.32 | convolution fusion | flops 3229089792 | bytes 7340032 | tf_op jit(solution)/shard_map/dot_general | solution.py:21
  90.6 0.0 reduce-scatter.3.cloned.1.call-update
  90.6 23.1 %reduce-scatter.5.cloned.1.call-done = bf16[960,256]{1,0:T(8,128)(2,1)} async-done(((bf16[960,1024]{1,0:T(8,128)(2,1)}), bf16[960,256]{1,0:T(8,128)(2,1)}) %reduce-scatter.5.cloned.1.call-update) | async-done | bytes 491536 | tf_op jit(solution)/shard_map/reduce_scatter | solution.py:50
  113.7 4.6 %all-to-all-start.1 = ((bf16[4,240,256]{2,1,0:T(8,128)(2,1)}), bf16[4,240,256]{2,1,0:T(8,128)(2,1)S(1)}, u32[]{:S(2)}, u32[]{:S(2)}) async-start(bf16[4,240,256]{2,1,0:T(8,128)(2,1)} %bitcast.21), calls=%async_computation.3 | async-start | bytes 983040 | tf_op jit(solution)/shard_map/all_to_all | solution.py:51
  118.3 25.8 %reduce-scatter.3.cloned.1.call-done = bf16[768,256]{1,0:T(8,128)(2,1)} async-done(((bf16[768,1024]{1,0:T(8,128)(2,1)}), bf16[768,256]{1,0:T(8,128)(2,1)}) %reduce-scatter.3.cloned.1.call-update) | async-done | bytes 393232 | tf_op jit(solution)/shard_map/reduce_scatter | solution.py:63
  144.2 0.0 all-to-all-done.1
  144.2 2.5 %fusion.40 = bf16[768,256]{1,0:T(8,128)(2,1)} fusion(bf16[960,256]{1,0:T(8,128)(2,1)S(1)} %bitcast.22, s32[768]{0:T(1024)S(1)} %add_select_fusion, bf16[768,256]{1,0:T(8,128)(2,1)} %reduce-scatter.3.cloned.1.call-done, f32[768]{0:T(1024)S(1)} %copy-done.3), kind=kOutput, calls=%fused_computation.42 | convolution fusion | flops 379011072 | bytes 1284096 | tf_op jit(solution)/shard_map/dot_general | solution.py:58
  (7 shorter events, 0.0 us)
Async XLA Ops:
  6.5 68.9 %copy-start = (bf16[1,1024,1024]{2,1,0:T(8,128)(2,1)S(1)}, bf16[1,1024,1024]{2,1,0:T(8,128)(2,1)}, u32[]{:S(2)}) copy-start(bf16[1,1024,1024]{2,1,0:T(8,128)(2,1)} %param.14) | copy-start | bytes 6291460
  6.5 24.9 %all-gather.3.cloned.1.call-start = ((), (), s32[]{:S(2)}) async-start(), calls=%async_computation.4 | async-start | bytes 1966080 | tf_op jit(solution)/shard_map/all_gather | solution.py:16
  7.3 68.1 %all-gather.5.cloned.1.call-start = ((), (), s32[]{:S(2)}) async-start(), calls=%async_computation.6 | async-start | bytes 2457600 | tf_op jit(solution)/shard_map/all_gather | solution.py:44
  31.5 1.9 %copy-start.1 = (bf16[768,1024]{1,0:T(8,128)(2,1)S(1)}, bf16[768,1024]{1,0:T(8,128)(2,1)}, u32[]{:S(2)}) copy-start(bf16[768,1024]{1,0:T(8,128)(2,1)} %all-gather.3.cloned.1.call-done) | copy-start | bytes 4718596
  34.5 1.1 copy-start.2
  55.0 58.7 %reduce-scatter.5.cloned.1.call-start = ((), (), s32[]{:S(2)}) async-start(), calls=%async_computation.7 | async-start | bytes 2457600 | tf_op jit(solution)/shard_map/reduce_scatter | solution.py:50
  83.2 61.0 %reduce-scatter.3.cloned.1.call-start = ((), (), s32[]{:S(2)}) async-start(), calls=%async_computation.5 | async-start | bytes 1966080 | tf_op jit(solution)/shard_map/reduce_scatter | solution.py:63
  90.6 53.6 %copy-start.3 = (f32[768]{0:T(1024)S(1)}, f32[768]{0:T(1024)}, u32[]{:S(2)}) copy-start(f32[768]{0:T(1024)} %param.17) | copy-start | bytes 9220
  113.7 30.5 %all-to-all-start.1 = ((bf16[4,240,256]{2,1,0:T(8,128)(2,1)}), bf16[4,240,256]{2,1,0:T(8,128)(2,1)S(1)}, u32[]{:S(2)}, u32[]{:S(2)}) async-start(bf16[4,240,256]{2,1,0:T(8,128)(2,1)} %bitcast.21), calls=%async_computation.3 | async-start | bytes 983040 | tf_op jit(solution)/shard_map/all_to_all | solution.py:51
Sparse Core Ops, SparseCore 0:
  8.9 22.5 all-gather.2
  55.2 20.1 all-gather.4
  83.3 30.3 reduce-scatter.4
  116.1 28.0 reduce-scatter.2
where the time goes:
time: 154 us; the launch traced here: 153 us
  waiting for transfers between devices  93.4 us (61%)
  blocking collectives  18.7 us (12%)
  matrix products  18.3 us (12%)
  between operations  13.2 us (9%)
  starting transfers between devices  4.75 us (3%)
  other arithmetic  3.73 us (2%)
    reduce_scatter x1, waiting for transfers between devices, per_device(): lax.psum_scatter(res_part.astype(jnp.bfloat16), 'mp', scatter_dimension=1...  25.8 us
    all_gather x1, waiting for transfers between devices, per_device(): full_rows = lax.all_gather(tokens, 'mp', axis=1, tiled=True)  23.4 us
    reduce_scatter x1, waiting for transfers between devices, per_device(): lax.psum_scatter(exp_part.astype(jnp.bfloat16), 'mp', scatter_dimension=1...  23.1 us
    all_gather x1, waiting for transfers between devices, per_device(): piece = lax.all_gather(incoming, 'mp', axis=2, tiled=True)  20.3 us
    all_to_all x1, blocking collectives, per_device(): lax.all_to_all(outgoing.reshape(experts, capacity, feat_width), 'expert',...  18.7 us
    dot_general x1, matrix products, per_device(): jnp.dot(exp_hidden, local_out, preferred_element_type=jnp.float32)  7.77 us
    dot_general x1, matrix products, per_device(): jnp.dot(res_hidden, w_res_out, preferred_element_type=jnp.float32)  7.35 us
    all_to_all x1, starting transfers between devices, per_device(): lax.all_to_all(summed.reshape(experts, capacity, feat_width), 'expert', s...  4.62 us
  transfers between devices with their start and end apart: 5, of which 4 were waited for; matrix products, arithmetic and copies ran while one was open for 5% of the time, Pallas kernels for 0%

commit v1 on v0

--- a/solution.py
+++ b/solution.py
@@ -13,7 +13,7 @@
 def per_device(
     tokens, gain, w_res_in, w_res_out, w_exp_in, w_exp_out, expert_of, slot_of, gate_prob
 ):
-    full_rows = lax.all_gather(tokens, "mp", axis=1, tiled=True)
+    full_rows = jnp.concatenate(lax.all_gather(tokens, "mp"), axis=1)
     normed = rms_rows(full_rows, gain)
     res_hidden = jax.nn.gelu(jnp.dot(normed, w_res_in, preferred_element_type=jnp.float32)).astype(
         jnp.bfloat16

time: 154 us -> 161 us (1.045)
  other arithmetic: 3.73 us -> 8.02 us
  local copies, waits for them, and re-layouts: 1.15 us -> 4.77 us
    convert_element_type x0 -> x1, local copies, waits for them, and re-layouts: none -> 3.58 us  [rms_rows(): values = tokens.astype(jnp.float32)]
    convert_element_type x0 -> x1, other arithmetic: none -> 3.32 us  [rms_rows(): values = tokens.astype(jnp.float32)]
where the time goes in v1:
time: 161 us
  waiting for transfers between devices  92.9 us (58%)
  matrix products  18.7 us (12%)
  blocking collectives  18.7 us (12%)
  between operations  13.2 us (8%)
  other arithmetic  8.02 us (5%)
  local copies, waits for them, and re-layouts  4.77 us (3%)
  starting transfers between devices  4.72 us (3%)
    reduce_scatter x1, waiting for transfers between devices, per_device(): lax.psum_scatter(res_part.astype(jnp.bfloat16), 'mp', scatter_dimension=1...  25.8 us
    all_gather x1, waiting for transfers between devices, per_device(): full_rows = jnp.concatenate(lax.all_gather(tokens, 'mp'), axis=1)  23.3 us
    reduce_scatter x1, waiting for transfers between devices, per_device(): lax.psum_scatter(exp_part.astype(jnp.bfloat16), 'mp', scatter_dimension=1...  22.7 us
    all_gather x1, waiting for transfers between devices, per_device(): piece = lax.all_gather(incoming, 'mp', axis=2, tiled=True)  20.3 us
    all_to_all x1, blocking collectives, per_device(): lax.all_to_all(outgoing.reshape(experts, capacity, feat_width), 'expert',...  18.7 us
    dot_general x1, matrix products, per_device(): jnp.dot(exp_hidden, local_out, preferred_element_type=jnp.float32)  7.81 us
    dot_general x1, matrix products, per_device(): jnp.dot(res_hidden, w_res_out, preferred_element_type=jnp.float32)  7.74 us
    all_to_all x1, starting transfers between devices, per_device(): lax.all_to_all(summed.reshape(experts, capacity, feat_width), 'expert', s...  4.6 us
  transfers between devices with their start and end apart: 5, of which 4 were waited for; matrix products, arithmetic and copies ran while one was open for 5% of the time, Pallas kernels for 0%

profile of v1, /device:TPU:0, one launch (start us, length us, event | category | flops | bytes accessed | tf_op | source)
XLA Modules:
  0.0 160.9 jit_solution(12388165496052242017)
XLA Ops:
  6.5 0.7 all-gather.6.cloned.1.call-update
  7.3 0.0 all-gather.4.cloned.1.call-start
  7.3 0.7 add_select_fusion
  8.0 23.3 %all-gather.6.cloned.1.call-done = bf16[3072,256]{1,0:T(8,128)(2,1)} async-done(((bf16[768,256]{1,0:T(8,128)(2,1)}), bf16[3072,256]{1,0:T(8,128)(2,1)}) %all-gather.6.cloned.1.call-update) | async-done | bytes 1572880 | tf_op jit(solution)/shard_map/all_gather | solution.py:16
  31.3 1.8 %fusion.8 = f32[768]{0:T(1024)S(1)} fusion(bf16[4,768,256]{2,1,0:T(8,128)(2,1)} %bitcast.31), kind=kLoop, calls=%fused_computation.12 | loop fusion | flops 2358528 | bytes 1575936 | tf_op jit(solution)/shard_map/reduce_sum | solution.py:9
  33.1 3.3 %convert_bitcast_fusion = f32[768,4,256]{2,0,1:T(8,128)} fusion(bf16[4,768,256]{2,1,0:T(8,128)(2,1)} %bitcast.32), kind=kLoop, calls=%fused_computation.11 | loop fusion | flops 786432 | bytes 4718592 | tf_op jit(solution)/shard_map/convert_element_type | solution.py:8
  36.4 3.6 %copy.10 = f32[768,4,256]{0,2,1:T(8,128)} copy(f32[768,4,256]{2,0,1:T(8,128)} %convert_bitcast_fusion) | data formatting | bytes 6291456 | tf_op jit(solution)/shard_map/convert_element_type | solution.py:8
  40.0 2.2 %fusion.18 = bf16[768,1024]{0,1:T(8,128)(2,1)S(1)} fusion(f32[768,4,256]{0,2,1:T(8,128)} %copy.10, f32[1024]{0:T(1024)S(1)} %copy-done.2, f32[768]{0:T(1024)S(1)} %add_rsqrt_fusion), kind=kLoop, calls=%fused_computation.23 | loop fusion | flops 2359296 | bytes 4725760 | tf_op jit(solution)/shard_map/convert_element_type | solution.py:10
  42.2 1.2 copy-done.1
  43.4 0.6 fusion.39
  44.0 18.7 %all_to_all.10 = bf16[4,240,256]{2,1,0:T(8,128)(2,1)} all-to-all(bf16[4,240,256]{2,1,0:T(8,128)(2,1)S(1)} %bitcast.35), channel_id=1, replica_groups=mesh['groups'=2,'expert'=4,'mp'=4] {'expert'}, dimensions={0} | all-to-all | bytes 983040 | tf_op jit(solution)/shard_map/all_to_all | solution.py:37
  62.7 0.0 all-gather.4.cloned.1.call-update
  62.7 0.0 reduce-scatter.5.cloned.1.call-start
  62.8 20.3 %all-gather.4.cloned.1.call-done = bf16[4,240,1024]{2,1,0:T(8,128)(2,1)} async-done(((bf16[4,240,256]{2,1,0:T(8,128)(2,1)}), bf16[4,240,1024]{2,1,0:T(8,128)(2,1)}) %all-gather.4.cloned.1.call-update) | async-done | bytes 1966096 | tf_op jit(solution)/shard_map/all_gather | solution.py:44
  83.1 7.8 %fusion.27 = bf16[960,1024]{1,0:T(8,128)(2,1)} fusion(bf16[1,1024,1024]{2,1,0:T(8,128)(2,1)S(1)} %copy-done, bf16[960,1024]{1,0:T(8,128)(2,1)} %bitcast.36, bf16[1,1024,1024]{2,1,0:T(8,128)(2,1)} %param.13), kind=kOutput, calls=%fused_computation.32 | convolution fusion | flops 4036362240 | bytes 8126464 | tf_op jit(solution)/shard_map/dot_general | solution.py:48
  90.9 0.0 reduce-scatter.5.cloned.1.call-update
  90.9 0.0 copy-start.3
  90.9 0.0 reduce-scatter.3.cloned.1.call-start
  91.0 7.7 %convolution_convert_fusion = bf16[768,1024]{1,0:T(8,128)(2,1)} fusion(bf16[1024,1024]{1,0:T(8,128)(2,1)} %param.12, bf16[768,1024]{0,1:T(8,128)(2,1)} %copy-done.1, bf16[1024,1024]{1,0:T(8,128)(2,1)} %param.11), kind=kOutput, calls=%fused_computation.33 | convolution fusion | flops 3229089792 | bytes 7340032 | tf_op jit(solution)/shard_map/dot_general | solution.py:21
  98.7 0.0 reduce-scatter.3.cloned.1.call-update
  98.7 22.7 %reduce-scatter.5.cloned.1.call-done = bf16[960,256]{1,0:T(8,128)(2,1)} async-done(((bf16[960,1024]{1,0:T(8,128)(2,1)}), bf16[960,256]{1,0:T(8,128)(2,1)}) %reduce-scatter.5.cloned.1.call-update) | async-done | bytes 491536 | tf_op jit(solution)/shard_map/reduce_scatter | solution.py:50
  121.5 4.6 %all-to-all-start.1 = ((bf16[4,240,256]{2,1,0:T(8,128)(2,1)}), bf16[4,240,256]{2,1,0:T(8,128)(2,1)S(1)}, u32[]{:S(2)}, u32[]{:S(2)}) async-start(bf16[4,240,256]{2,1,0:T(8,128)(2,1)} %bitcast.33), calls=%async_computation.3 | async-start | bytes 983040 | tf_op jit(solution)/shard_map/all_to_all | solution.py:51
  126.0 25.8 %reduce-scatter.3.cloned.1.call-done = bf16[768,256]{1,0:T(8,128)(2,1)} async-done(((bf16[768,1024]{1,0:T(8,128)(2,1)}), bf16[768,256]{1,0:T(8,128)(2,1)}) %reduce-scatter.3.cloned.1.call-update) | async-done | bytes 393232 | tf_op jit(solution)/shard_map/reduce_scatter | solution.py:63
  151.9 2.5 %fusion.40 = bf16[768,256]{1,0:T(8,128)(2,1)} fusion(bf16[960,256]{1,0:T(8,128)(2,1)S(1)} %bitcast.34, s32[768]{0:T(1024)S(1)} %add_select_fusion, bf16[768,256]{1,0:T(8,128)(2,1)} %reduce-scatter.3.cloned.1.call-done, f32[768]{0:T(1024)S(1)} %copy-done.3), kind=kOutput, calls=%fused_computation.43 | convolution fusion | flops 379011072 | bytes 1284096 | tf_op jit(solution)/shard_map/dot_general | solution.py:58
  (9 shorter events, 0.0 us)
Async XLA Ops:
  6.5 76.5 %copy-start = (bf16[1,1024,1024]{2,1,0:T(8,128)(2,1)S(1)}, bf16[1,1024,1024]{2,1,0:T(8,128)(2,1)}, u32[]{:S(2)}) copy-start(bf16[1,1024,1024]{2,1,0:T(8,128)(2,1)} %param.14) | copy-start | bytes 6291460
  6.5 24.7 %all-gather.6.cloned.1.call-start = ((), (), s32[]{:S(2)}) async-start(), calls=%async_computation.7 | async-start | bytes 1966080 | tf_op jit(solution)/shard_map/all_gather | solution.py:16
  7.3 75.8 %all-gather.4.cloned.1.call-start = ((), (), s32[]{:S(2)}) async-start(), calls=%async_computation.5 | async-start | bytes 2457600 | tf_op jit(solution)/shard_map/all_gather | solution.py:44
  36.4 3.6 %copy-start.2 = (f32[1024]{0:T(1024)S(1)}, f32[1024]{0:T(1024)}, u32[]{:S(2)}) copy-start(f32[1024]{0:T(1024)} %param.10) | copy-start | bytes 12292
  42.2 1.2 copy-start.1
  62.7 58.7 %reduce-scatter.5.cloned.1.call-start = ((), (), s32[]{:S(2)}) async-start(), calls=%async_computation.6 | async-start | bytes 2457600 | tf_op jit(solution)/shard_map/reduce_scatter | solution.py:50
  90.9 61.0 %copy-start.3 = (f32[768]{0:T(1024)S(1)}, f32[768]{0:T(1024)}, u32[]{:S(2)}) copy-start(f32[768]{0:T(1024)} %param.17) | copy-start | bytes 9220
  90.9 60.9 %reduce-scatter.3.cloned.1.call-start = ((), (), s32[]{:S(2)}) async-start(), calls=%async_computation.4 | async-start | bytes 1966080 | tf_op jit(solution)/shard_map/reduce_scatter | solution.py:63
  121.5 30.4 %all-to-all-start.1 = ((bf16[4,240,256]{2,1,0:T(8,128)(2,1)}), bf16[4,240,256]{2,1,0:T(8,128)(2,1)S(1)}, u32[]{:S(2)}, u32[]{:S(2)}) async-start(bf16[4,240,256]{2,1,0:T(8,128)(2,1)} %bitcast.33), calls=%async_computation.3 | async-start | bytes 983040 | tf_op jit(solution)/shard_map/all_to_all | solution.py:51
Sparse Core Ops, SparseCore 0:
  8.9 22.3 all-gather.5
  62.8 20.1 all-gather.3
  91.0 30.3 reduce-scatter.4
  123.8 27.9 reduce-scatter.2
